TPU v7x, 32 devices: a whole 2x2x4 slice. The times are simulated.
32 devices in a mesh: prow: 8 (over z, x), pcol: 4 (over y, core).
Axes of the slice: x: 2, y: 2, z: 4, core: 2. Of those that a mesh axis runs over, the one named last changes fastest.
Arguments:
- a_matrix: bfloat16 [32768, 512], P('prow', 'pcol'), may hold values from -6 to 6
- l_panel: bfloat16 [32768, 256], P('prow', 'pcol'), may hold values from -0.375 to 0.375
- l_inverse: bfloat16 [256, 256], replicated, may hold values from -1 to 1
- pivots: int32 [256], replicated, may hold values from 0 to 32767, as said below
Outputs:
- updated: bfloat16 [32768, 512], P('prow', 'pcol')
Inputs may be any that keep to these rules, and one draw needn't show every extreme that they name: pivots[j] >= j for every j.
All inputs are finite; a program needn't handle non-finite values.
Results may differ from a plain program's by a relative error of at most 0.0039.
Values may be sent and summed in bfloat16 or wider, within the bound.
A program may use at most 64 MiB of HBM per device.

v0:
```python
import functools

import jax
import jax.numpy as jnp
from jax import lax
from jax.experimental import pallas as pl
from jax.experimental.pallas import tpu as pltpu
from jax.sharding import PartitionSpec as P

MESH = pl.DeviceIdType.MESH
F32 = jnp.float32
BF16 = jnp.bfloat16
CORES = 2


def one_hot(mask):
    return jnp.where(mask, 1.0, 0.0).astype(BF16)


def swap_plan(pv_row):
    nb = pv_row.shape[1]
    slot = lax.broadcasted_iota(jnp.int32, (nb, nb), 0).astype(F32)
    other = lax.broadcasted_iota(jnp.int32, (nb, nb), 1).astype(F32)
    slot_col = lax.broadcasted_iota(jnp.int32, (nb, 1), 0).astype(F32)
    earlier = other < slot
    pv_col = jnp.max(jnp.where(slot == other, pv_row, -1.0), axis=1, keepdims=True)
    pointer = jnp.max(jnp.where((pv_row == slot) & earlier, other, -1.0), axis=1, keepdims=True)
    chain = one_hot(other == jnp.where(pointer >= 0, pointer, slot_col))
    for _ in range((nb - 1).bit_length()):
        chain = jnp.dot(chain, chain, preferred_element_type=F32).astype(BF16)
    same = pv_row == pv_col
    previous = jnp.max(jnp.where(same & earlier, other, -1.0), axis=1, keepdims=True)
    via = jnp.dot(one_hot(other == previous), chain, preferred_element_type=F32)
    via_chain = jnp.max(jnp.where(via > 0.5, other, -1.0), axis=1, keepdims=True)
    top_source = jnp.where(previous >= 0, via_chain, pv_col)
    repeated = jnp.max(jnp.where(same & (slot > other), 1.0, 0.0), axis=0, keepdims=True)
    landing = jnp.where((repeated < 0.5) & (pv_row >= nb), pv_row, -1.0)
    return top_source, chain, landing


def kernel(
    n_prow, n_pcol, chunks,
    a_hbm, l_hbm, inv_hbm, pv_hbm, out_v,
    a_v, l_full, inv_v, pv_ref, part, got, mine, tops, origs,
    load_sem,
    p1_send, p1_recv, p2_send, p2_recv, o1_send, o1_recv, o2_send, o2_recv,
    y_send, y_recv, m_send, m_recv, f_send, f_recv,
):
    rows, width = a_v.shape
    nb = inv_v.shape[0]
    n_red, piece, _ = part.shape
    step = rows // chunks
    n_y = n_pcol // CORES
    me = lax.axis_index("prow")
    col = lax.axis_index("pcol")
    y, core = col // CORES, col % CORES
    mate = y * CORES + (1 - core)

    def y_peer(d):
        return lax.rem(y + d, n_y) * CORES + core

    def y_from(d):
        return lax.rem(y + n_y - d, n_y) * CORES + core

    def to(d):
        return lax.rem(me + d, n_prow)

    def frm(d):
        return lax.rem(me + n_prow - d, n_prow)

    first = (n_prow - n_red) // 2

    def is_red(index):
        return (index >= first) & (index < first + n_red)

    def if_red(index, fn):
        pl.when(is_red(index))(fn)

    def slot_of(index):
        return lax.rem(index + n_prow - first, n_red)

    l_load = pltpu.make_async_copy(l_hbm, l_full.at[col], load_sem.at[0])
    a_load = pltpu.make_async_copy(a_hbm, a_v, load_sem.at[1])
    inv_load = pltpu.make_async_copy(inv_hbm, inv_v, load_sem.at[2])
    pv_load = pltpu.make_async_copy(pv_hbm, pv_ref, load_sem.at[3])
    pv_load.start()
    l_load.start()
    a_load.start()
    inv_load.start()

    barrier = pltpu.get_barrier_semaphore()
    for d in range(1, n_prow):
        @pl.when(is_red(me) | is_red(to(d)))
        def _():
            pl.semaphore_signal(barrier, inc=1, device_id=(to(d), col), device_id_type=MESH)
    for d in range(1, n_y):
        pl.semaphore_signal(barrier, inc=1, device_id=(me, y_peer(d)), device_id_type=MESH)
    pl.semaphore_signal(barrier, inc=1, device_id=(me, mate), device_id_type=MESH)

    pv_load.wait()
    top_source, chain, landing = swap_plan(pv_ref[...].astype(F32))

    l_load.wait()
    pl.semaphore_wait(barrier, n_y + jnp.where(is_red(me), n_prow - 1, n_red))

    def cols(k):
        return pl.ds(k * step, step)

    y_copies = {}
    for k in range(chunks):
        for d in range(1, n_y):
            y_copies[d, k] = pltpu.make_async_remote_copy(
                l_full.at[col, :, cols(k)], l_full.at[col, :, cols(k)],
                y_send.at[d, k], y_recv.at[d, k], device_id=(me, y_peer(d)), device_id_type=MESH)
            y_copies[d, k].start()
    m_copy = pltpu.make_async_remote_copy(
        l_full.at[col], l_full.at[col], m_send, m_recv, device_id=(me, mate), device_id_type=MESH)

    a_load.wait()
    o1_copies = [
        pltpu.make_async_remote_copy(
            a_v.at[pl.ds(d * piece, piece)], origs.at[d], o1_send.at[d], o1_recv,
            device_id=(first + d, col), device_id_type=MESH)
        for d in range(n_red)
    ]

    @pl.when(me == 0)
    def _():
        for copy in o1_copies:
            copy.start()

    m_copy.start()

    def global_rows(shape, axis, start):
        local = lax.broadcasted_iota(jnp.int32, shape, axis) + start
        return ((local // nb * n_prow + me) * nb + local % nb).astype(F32)

    total = jnp.zeros((nb, width), F32)
    for k in range(chunks):
        pick = one_hot(top_source == global_rows((1, step), 1, k * step))
        total = total + jnp.dot(pick, a_v[pl.ds(k * step, step), :], preferred_element_type=F32)
    part[...] = total.astype(BF16).reshape(n_red, piece, width)

    p1_copies = {}
    for d in range(1, n_prow):
        t = to(d)
        p1_copies[d] = pltpu.make_async_remote_copy(
            part.at[slot_of(t)], got.at[d], p1_send.at[d], p1_recv.at[d],
            device_id=(t, col), device_id_type=MESH)
        if_red(t, p1_copies[d].start)

    f_copies = {}

    def forward(k):
        for d in range(1, n_y):
            y_copies[d, k].wait_recv()
            src = y_from(d)
            f_copies[d, k] = pltpu.make_async_remote_copy(
                l_full.at[src, :, cols(k)], l_full.at[src, :, cols(k)],
                f_send.at[d, k], f_recv.at[d, k], device_id=(me, mate), device_id_type=MESH)
            f_copies[d, k].start()

    slot = slot_of(me)
    o2_copies, p2_copies = {}, {}
    for d in range(1, n_prow):
        o2_copies[d] = pltpu.make_async_remote_copy(
            origs.at[slot], origs.at[slot], o2_send.at[d], o2_recv.at[d],
            device_id=(to(d), col), device_id_type=MESH)
        p2_copies[d] = pltpu.make_async_remote_copy(
            mine, tops.at[slot], p2_send.at[d], p2_recv.at[d],
            device_id=(to(d), col), device_id_type=MESH)

    def send_orig():
        o1_copies[0].wait_recv()
        for d in range(1, n_prow):
            o2_copies[d].start()

    if_red(me, send_orig)
    forward(0)
    forward(1)

    def reduce_and_send():
        acc = part[slot].astype(F32)
        for d in range(1, n_prow):
            p1_copies[d].wait_recv()
            acc = acc + got[d].astype(F32)
        mine[...] = acc.astype(BF16)
        tops[slot] = acc.astype(BF16)
        for d in range(1, n_prow):
            p2_copies[d].start()

    if_red(me, reduce_and_send)
    forward(2)

    for d in range(1, n_prow):
        if_red(frm(d), o2_copies[d].wait_recv)
    moved = jnp.dot(chain, origs[...].reshape(nb, width), preferred_element_type=F32).astype(BF16)
    moved = jnp.concatenate([moved, jnp.ones((nb, width), BF16)], axis=1)
    for k in range(chunks):
        here = one_hot(landing == global_rows((step, 1), 0, k * step))
        both = jnp.dot(here, moved, preferred_element_type=F32)
        rows_k = pl.ds(k * step, step)
        out_v[rows_k, :] = jnp.where(
            both[:, width:] > 0.5, both[:, :width], a_v[rows_k, :].astype(F32)).astype(BF16)

    early = min(5, chunks)
    for k in range(3, early):
        forward(k)
    for d in range(1, n_prow):
        if_red(frm(d), p2_copies[d].wait_recv)
    inv_load.wait()
    u_block = jnp.dot(
        inv_v[...], tops[...].reshape(nb, width), preferred_element_type=F32).astype(BF16)

    def finish(k):
        for d in range(1, n_y):
            f_copies[d, k].wait_recv()
        rows_k = pl.ds(k * step, step)
        panel = l_full[:, :, cols(k)].reshape(nb, step)
        update = lax.dot_general(
            panel, u_block, (((0,), (0,)), ((), ())), preferred_element_type=F32)
        out_v[rows_k, :] = (out_v[rows_k, :].astype(F32) - update).astype(BF16)
        top = min(step, nb - k * step)
        if top > 0:
            @pl.when(me == 0)
            def _():
                out_v[pl.ds(k * step, top), :] = u_block[k * step:k * step + top, :]

    m_copy.wait_recv()
    done = 0
    for k in range(early, chunks):
        forward(k)
        while done < k:
            finish(done)
            done += 1
    for k in range(done, chunks):
        finish(k)

    @pl.when(me == 0)
    def _():
        for copy in o1_copies:
            copy.wait_send()

    m_copy.wait_send()
    for d in range(1, n_prow):
        if_red(to(d), p1_copies[d].wait_send)

    def drain():
        for d in range(1, n_prow):
            o2_copies[d].wait_send()
            p2_copies[d].wait_send()

    if_red(me, drain)
    for key in y_copies:
        y_copies[key].wait_send()
        f_copies[key].wait_send()


def hbm(array):
    return pltpu.with_memory_space_constraint(array, pltpu.HBM)


def body(n_prow, n_pcol, a_matrix, l_panel, l_inverse, pivots):
    rows, width = a_matrix.shape
    nb = l_inverse.shape[0]
    depth = l_panel.shape[1]
    n_red = min(n_prow // 2, nb // 16)
    piece = nb // n_red
    n_y = n_pcol // CORES
    chunks = min(8, rows // 128)
    dma = pltpu.SemaphoreType.DMA
    return pl.pallas_call(
        functools.partial(kernel, n_prow, n_pcol, chunks),
        out_shape=jax.ShapeDtypeStruct((rows, width), BF16),
        in_specs=[pl.BlockSpec(memory_space=pl.ANY)] * 4,
        out_specs=pl.BlockSpec(memory_space=pltpu.VMEM),
        scratch_shapes=[
            pltpu.VMEM((rows, width), BF16),
            pltpu.VMEM((n_pcol, depth, rows), BF16),
            pltpu.VMEM((nb, nb), BF16),
            pltpu.VMEM((1, nb), jnp.int32),
            pltpu.VMEM((n_red, piece, width), BF16),
            pltpu.VMEM((n_prow, piece, width), BF16),
            pltpu.VMEM((piece, width), BF16),
            pltpu.VMEM((n_red, piece, width), BF16),
            pltpu.VMEM((n_red, piece, width), BF16),
            dma((4,)),
            dma((n_prow,)), dma((n_prow,)), dma((n_prow,)), dma((n_prow,)),
            dma((n_red,)), dma, dma((n_prow,)), dma((n_prow,)),
            dma((n_y, chunks)), dma((n_y, chunks)), dma, dma,
            dma((n_y, chunks)), dma((n_y, chunks)),
        ],
        compiler_params=pltpu.CompilerParams(
            collective_id=0, has_side_effects=True, vmem_limit_bytes=24 * 2 ** 20),
    )(hbm(a_matrix), hbm(l_panel.T), hbm(l_inverse), hbm(pivots.reshape(1, nb)))


def solution(mesh):
    n_prow, n_pcol = mesh.shape["prow"], mesh.shape["pcol"]
    in_specs = (P("prow", "pcol"), P("prow", "pcol"), P(), P())
    return jax.shard_map(
        functools.partial(body, n_prow, n_pcol),
        mesh=mesh, in_specs=in_specs, out_specs=P("prow", "pcol"), check_vma=False)
```

profile of v0, /device:TPU:0, one launch (start us, length us, event | category | flops | bytes accessed | tf_op | source)
XLA Modules:
  0.0 21.3 jit_solution(13457757551443347391)
XLA Ops:
  0.0 20.3 %shard_map.46 = bf16[4096,128]{1,0:T(8,128)(2,1)S(1)} custom-call(bf16[4096,128]{1,0:T(8,128)(2,1)} %a_hbm.1, bf16[64,4096]{1,0:T(8,128)(2,1)} %bitcast.2, bf16[256,256]{1,0:T(8,128)(2,1)} %inv_hbm.1, s32[1,256]{1,0:T(1,128)} %bitcast.3), custom_call_target="tpu_custom_call" | custom-call | tf_op jit(solution)/shard_map/pallas_call | solution.py:272
  20.3 1.0 %copy.6 = bf16[4096,128]{1,0:T(8,128)(2,1)} copy(bf16[4096,128]{1,0:T(8,128)(2,1)S(1)} %shard_map.46) | data formatting | bytes 2097152
where the time goes:
time: 21.7 us; the launch traced here: 21.3 us
  Pallas kernels  20.3 us (94%)
  local copies, waits for them, and re-layouts  0.97 us (4%)
    pallas_call x1, Pallas kernels, body(): pl.pallas_call(functools.partial(kernel, n_prow, n_pcol, chunks), out_sha...  20.3 us
    unnamed x1, local copies, waits for them, and re-layouts  0.97 us

commit v1 on v0

v1 whole, which is shorter than its diff:
```python
import functools

import jax
import jax.numpy as jnp
from jax import lax
from jax.experimental import pallas as pl
from jax.experimental.pallas import tpu as pltpu
from jax.sharding import PartitionSpec as P

MESH = pl.DeviceIdType.MESH
F32 = jnp.float32
BF16 = jnp.bfloat16
CORES = 2
LOADS = 4


def one_hot(mask):
    return jnp.where(mask, 1.0, 0.0).astype(BF16)


def column_of(pv_row):
    nb = pv_row.shape[1]
    slot = lax.broadcasted_iota(jnp.int32, (nb, nb), 0)
    other = lax.broadcasted_iota(jnp.int32, (nb, nb), 1)
    return jnp.max(jnp.where(slot == other, pv_row, -1.0), axis=1, keepdims=True)


def swap_plan(pv_row, pv_col):
    nb = pv_row.shape[1]
    slot = lax.broadcasted_iota(jnp.int32, (nb, nb), 0).astype(F32)
    other = lax.broadcasted_iota(jnp.int32, (nb, nb), 1).astype(F32)
    slot_col = lax.broadcasted_iota(jnp.int32, (nb, 1), 0).astype(F32)
    earlier = other < slot
    pointer = jnp.max(jnp.where((pv_row == slot) & earlier, other, -1.0), axis=1, keepdims=True)
    chain = one_hot(other == jnp.where(pointer >= 0, pointer, slot_col))
    for _ in range((nb - 1).bit_length()):
        chain = jnp.dot(chain, chain, preferred_element_type=F32).astype(BF16)
    same = pv_row == pv_col
    previous = jnp.max(jnp.where(same & earlier, other, -1.0), axis=1, keepdims=True)
    via = jnp.dot(one_hot(other == previous), chain, preferred_element_type=F32).astype(BF16)
    repeated = jnp.max(jnp.where(same & (slot > other), 1.0, 0.0), axis=0, keepdims=True)
    landing = jnp.where((repeated < 0.5) & (pv_row >= nb), pv_row, -1.0)
    return previous, via, chain, landing


def kernel(
    n_prow, n_pcol, bounds,
    a_hbm, l_hbm, inv_hbm, pv_hbm, out_v,
    a_v, l_full, inv_v, pv_ref, part, got, mine, tops, origs,
    load_sem, a_sem,
    p1_send, p1_recv, p2_send, p2_recv, o1_send, o1_recv, o2_send, o2_recv, o_here,
    y_send, y_recv, m_send, m_recv, f_send, f_recv,
    owner_up, rest_up, mate_in,
):
    rows, width = a_v.shape
    nb = inv_v.shape[0]
    n_red, piece, _ = part.shape
    n_y = n_pcol // CORES
    chunks = len(bounds) - 1
    me = lax.axis_index("prow")
    col = lax.axis_index("pcol")
    y, core = col // CORES, col % CORES
    mate = y * CORES + (1 - core)

    def y_peer(d):
        return lax.rem(y + d, n_y) * CORES + core

    def y_from(d):
        return lax.rem(y + n_y - d, n_y) * CORES + core

    def to(d):
        return lax.rem(me + d, n_prow)

    def frm(d):
        return lax.rem(me + n_prow - d, n_prow)

    def lower(d):
        return me + d >= n_prow

    def is_red(index):
        return index < n_red

    def if_red(index, fn):
        pl.when(is_red(index))(fn)

    slot = lax.rem(me, n_red)

    barrier = pltpu.get_barrier_semaphore()
    for d in range(1, n_y):
        pl.semaphore_signal(barrier, inc=1, device_id=(me, y_peer(d)), device_id_type=MESH)

    @pl.when(core == 1)
    def _():
        pl.semaphore_signal(barrier, inc=1, device_id=(me, mate), device_id_type=MESH)

    for d in range(1, n_prow):
        @pl.when(is_red(me) & jnp.logical_not(lower(d)))
        def _():
            pl.semaphore_signal(barrier, inc=1, device_id=(to(d), col), device_id_type=MESH)

    pv_load = pltpu.make_async_copy(pv_hbm, pv_ref, load_sem.at[0])
    pv_load.start()
    block = rows // LOADS
    a_loads = [
        pltpu.make_async_copy(
            a_hbm.at[pl.ds(k * block, block)], a_v.at[pl.ds(k * block, block)], a_sem.at[k])
        for k in range(LOADS)
    ]
    for load in a_loads:
        load.start()
    l_load = pltpu.make_async_copy(l_hbm, l_full.at[col], load_sem.at[1])
    inv_load = pltpu.make_async_copy(inv_hbm, inv_v, load_sem.at[2])

    def cols(k):
        return pl.ds(bounds[k], bounds[k + 1] - bounds[k])

    def sent(k, fn):
        if bounds[k + 1] <= nb:
            pl.when(me > 0)(fn)
        else:
            fn()

    y_copies = {}
    for k in range(chunks):
        for d in range(1, n_y):
            y_copies[d, k] = pltpu.make_async_remote_copy(
                l_hbm.at[:, cols(k)], l_full.at[col, :, cols(k)],
                y_send.at[d, k], y_recv.at[d, k], device_id=(me, y_peer(d)), device_id_type=MESH)
    m_copy = pltpu.make_async_remote_copy(
        l_hbm, l_full.at[col], m_send, m_recv, device_id=(me, mate), device_id_type=MESH)

    def enter():
        pl.semaphore_wait(
            barrier, n_y - 1 + jnp.minimum(me, n_red) + jnp.where(core == 0, 1, 0))
        for k in range(chunks):
            for d in range(1, n_y):
                sent(k, y_copies[d, k].start)
        for d in range(1, n_prow):
            @pl.when(is_red(me) & lower(d))
            def _():
                pl.semaphore_signal(owner_up, inc=1, device_id=(to(d), col), device_id_type=MESH)

            @pl.when(jnp.logical_not(is_red(me)) & is_red(to(d)))
            def _():
                pl.semaphore_signal(rest_up, inc=1, device_id=(to(d), col), device_id_type=MESH)

        @pl.when(core == 0)
        def _():
            pl.semaphore_signal(mate_in, inc=1, device_id=(me, mate), device_id_type=MESH)
            m_copy.start()

    pl.when(is_red(me))(enter)
    l_load.start()
    inv_load.start()

    def global_rows(shape, axis, start):
        local = lax.broadcasted_iota(jnp.int32, shape, axis) + start
        return ((local // nb * n_prow + me) * nb + local % nb).astype(F32)

    pv_load.wait()
    pv_row = pv_ref[...].astype(F32)
    pv_col = column_of(pv_row)
    total = jnp.zeros((nb, width), F32)
    for k in range(LOADS):
        a_loads[k].wait()
        pick = one_hot(pv_col == global_rows((1, block), 1, k * block))
        total = total + jnp.dot(pick, a_v[pl.ds(k * block, block), :], preferred_element_type=F32)
    part[...] = total.astype(BF16).reshape(n_red, piece, width)

    pl.when(jnp.logical_not(is_red(me)))(enter)

    p1_copies = {}
    for d in range(1, n_prow):
        t = to(d)
        p1_copies[d] = pltpu.make_async_remote_copy(
            part.at[lax.rem(t, n_red)], got.at[d], p1_send.at[d], p1_recv.at[d],
            device_id=(t, col), device_id_type=MESH)
        pl.when(is_red(t) & lower(d))(p1_copies[d].start)

    @pl.when(me < n_red - 1)
    def _():
        pl.semaphore_wait(owner_up, n_red - 1 - me)

    o1_copies = [
        pltpu.make_async_remote_copy(
            a_v.at[pl.ds(t * piece, piece)], origs.at[t], o1_send.at[t], o1_recv,
            device_id=(t, col), device_id_type=MESH)
        for t in range(1, n_red)
    ]
    o_locals = [
        pltpu.make_async_copy(a_v.at[pl.ds(t * piece, piece)], origs.at[t], o_here.at[t])
        for t in range(n_red)
    ]

    @pl.when(me == 0)
    def _():
        for copy in o_locals:
            copy.start()
        for copy in o1_copies:
            copy.start()

    for d in range(1, n_prow):
        pl.when(is_red(to(d)) & jnp.logical_not(lower(d)))(p1_copies[d].start)

    @pl.when(core == 1)
    def _():
        pl.semaphore_wait(mate_in, 1)
        m_copy.start()

    previous, via, chain, landing = swap_plan(pv_row, pv_col)

    f_copies = {}
    for k in range(chunks):
        for d in range(1, n_y):
            src = y_from(d)
            f_copies[d, k] = pltpu.make_async_remote_copy(
                l_full.at[src, :, cols(k)], l_full.at[src, :, cols(k)],
                f_send.at[d, k], f_recv.at[d, k], device_id=(me, mate), device_id_type=MESH)

    def forward(k):
        if k >= chunks:
            return

        def go():
            for d in range(1, n_y):
                y_copies[d, k].wait_recv()
                f_copies[d, k].start()

        sent(k, go)

    o2_copies, p2_copies = {}, {}
    for d in range(1, n_prow):
        o2_copies[d] = pltpu.make_async_remote_copy(
            origs.at[slot], origs.at[slot], o2_send.at[d], o2_recv.at[d],
            device_id=(to(d), col), device_id_type=MESH)
        p2_copies[d] = pltpu.make_async_remote_copy(
            mine, tops.at[slot], p2_send.at[d], p2_recv.at[d],
            device_id=(to(d), col), device_id_type=MESH)

    def not_first(d, fn):
        pl.when(me + d != n_prow)(fn)

    def send_orig():
        @pl.when(me == 0)
        def _():
            for copy in o_locals:
                copy.wait()

        @pl.when(me > 0)
        def _():
            pltpu.make_async_remote_copy(
                a_v.at[pl.ds(0, piece)], origs.at[slot], o1_send.at[0], o1_recv,
                device_id=(0, col), device_id_type=MESH).wait_recv()

        pl.semaphore_wait(rest_up, n_prow - n_red)
        for d in range(1, n_prow):
            not_first(d, o2_copies[d].start)

    forward(0)
    if_red(me, send_orig)
    forward(1)
    forward(2)

    def reduce_and_send():
        acc = part[slot].astype(F32)
        for d in range(1, n_prow):
            p1_copies[d].wait_recv()
            acc = acc + got[d].astype(F32)
        mine[...] = acc.astype(BF16)
        tops[slot] = acc.astype(BF16)
        for d in range(1, n_prow):
            p2_copies[d].start()

    if_red(me, reduce_and_send)
    forward(3)

    @pl.when(me > 0)
    def _():
        for d in range(1, n_prow):
            if_red(frm(d), o2_copies[d].wait_recv)

    orig = origs[...].reshape(nb, width)
    moved = jnp.dot(chain, orig, preferred_element_type=F32).astype(BF16)
    again = jnp.dot(via, orig, preferred_element_type=F32).astype(BF16)
    moved = jnp.concatenate([moved, jnp.ones((nb, width), BF16)], axis=1)
    step = min(512, rows)
    for start in range(0, rows, step):
        here = one_hot(landing == global_rows((step, 1), 0, start))
        both = jnp.dot(here, moved, preferred_element_type=F32)
        rows_k = pl.ds(start, step)
        out_v[rows_k, :] = jnp.where(
            both[:, width:] > 0.5, both[:, :width], a_v[rows_k, :].astype(F32)).astype(BF16)

    forward(4)
    for d in range(1, n_prow):
        if_red(frm(d), p2_copies[d].wait_recv)
    inv_load.wait()
    top_rows = jnp.where(previous >= 0, again, tops[...].reshape(nb, width))
    u_block = jnp.dot(inv_v[...], top_rows, preferred_element_type=F32).astype(BF16)

    def arrived(k):
        def go():
            for d in range(1, n_y):
                f_copies[d, k].wait_recv()
        sent(k, go)

    def update(first, last):
        for k in range(first, last):
            arrived(k)
        start, stop = bounds[first], bounds[last]
        rows_k = pl.ds(start, stop - start)
        panel = l_full[:, :, rows_k].reshape(nb, stop - start)
        product = lax.dot_general(
            panel, u_block, (((0,), (0,)), ((), ())), preferred_element_type=F32)
        out_v[rows_k, :] = (out_v[rows_k, :].astype(F32) - product).astype(BF16)

    def top_update(k):
        @pl.when(me > 0)
        def _():
            update(k, k + 1)

        @pl.when(me == 0)
        def _():
            rows_k = cols(k)
            out_v[rows_k, :] = u_block[bounds[k]:bounds[k + 1], :]

    top = sum(1 for k in range(chunks) if bounds[k + 1] <= nb)
    m_copy.wait_recv()
    l_load.wait()
    for k in range(5, chunks - 2):
        forward(k)
    for k in range(top):
        top_update(k)
    mid = max(top, chunks - 4)
    if mid > top:
        update(top, mid)
    forward(chunks - 2) if chunks - 2 >= 5 else None
    late = max(mid, chunks - 2)
    if late > mid:
        update(mid, late)
    forward(chunks - 1) if chunks - 1 >= 5 else None
    for k in range(late, chunks):
        update(k, k + 1)

    @pl.when(me == 0)
    def _():
        for copy in o1_copies:
            copy.wait_send()

    m_copy.wait_send()
    for d in range(1, n_prow):
        if_red(to(d), p1_copies[d].wait_send)

    def drain():
        for d in range(1, n_prow):
            not_first(d, o2_copies[d].wait_send)
            p2_copies[d].wait_send()

    if_red(me, drain)
    for d, k in y_copies:
        sent(k, y_copies[d, k].wait_send)
        sent(k, f_copies[d, k].wait_send)


def hbm(array):
    return pltpu.with_memory_space_constraint(array, pltpu.HBM)


def chunk_bounds(rows, nb):
    bounds = [0, nb]
    while bounds[-1] < rows:
        bounds.append(min(bounds[-1] + 2 * nb, rows))
    return tuple(bounds)


def body(n_prow, n_pcol, a_matrix, l_panel, l_inverse, pivots):
    rows, width = a_matrix.shape
    nb = l_inverse.shape[0]
    depth = l_panel.shape[1]
    n_red = min(n_prow // 2, nb // 16)
    piece = nb // n_red
    n_y = n_pcol // CORES
    bounds = chunk_bounds(rows, nb)
    chunks = len(bounds) - 1
    dma = pltpu.SemaphoreType.DMA
    flag = pltpu.SemaphoreType.REGULAR
    return pl.pallas_call(
        functools.partial(kernel, n_prow, n_pcol, bounds),
        out_shape=jax.ShapeDtypeStruct((rows, width), BF16),
        in_specs=[pl.BlockSpec(memory_space=pl.ANY)] * 4,
        out_specs=pl.BlockSpec(memory_space=pltpu.VMEM),
        scratch_shapes=[
            pltpu.VMEM((rows, width), BF16),
            pltpu.VMEM((n_pcol, depth, rows), BF16),
            pltpu.VMEM((nb, nb), BF16),
            pltpu.VMEM((1, nb), jnp.int32),
            pltpu.VMEM((n_red, piece, width), BF16),
            pltpu.VMEM((n_prow, piece, width), BF16),
            pltpu.VMEM((piece, width), BF16),
            pltpu.VMEM((n_red, piece, width), BF16),
            pltpu.VMEM((n_red, piece, width), BF16),
            dma((3,)), dma((LOADS,)),
            dma((n_prow,)), dma((n_prow,)), dma((n_prow,)), dma((n_prow,)),
            dma((n_red,)), dma, dma((n_prow,)), dma((n_prow,)), dma((n_red,)),
            dma((n_y, chunks)), dma((n_y, chunks)), dma, dma,
            dma((n_y, chunks)), dma((n_y, chunks)),
            flag, flag, flag,
        ],
        compiler_params=pltpu.CompilerParams(
            collective_id=0, has_side_effects=True, vmem_limit_bytes=24 * 2 ** 20),
    )(hbm(a_matrix), hbm(l_panel.T), hbm(l_inverse), hbm(pivots.reshape(1, nb)))


def solution(mesh):
    n_prow, n_pcol = mesh.shape["prow"], mesh.shape["pcol"]
    in_specs = (P("prow", "pcol"), P("prow", "pcol"), P(), P())
    return jax.shard_map(
        functools.partial(body, n_prow, n_pcol),
        mesh=mesh, in_specs=in_specs, out_specs=P("prow", "pcol"), check_vma=False)
```

time: 21.7 us -> 19.9 us (0.917)
  the two profiles are of different devices: /device:TPU:0 before, /device:TPU:27 now
where the time goes in v1:
time: 19.9 us; the launch traced here: 19.8 us
  Pallas kernels  18.8 us (94%)
  local copies, waits for them, and re-layouts  0.97 us (5%)
    pallas_call x1, Pallas kernels, body(): pl.pallas_call(functools.partial(kernel, n_prow, n_pcol, bounds), out_sha...  18.8 us
    unnamed x1, local copies, waits for them, and re-layouts  0.97 us

profile of v1, /device:TPU:27, one launch (start us, length us, event | category | flops | bytes accessed | tf_op | source)
XLA Modules:
  0.0 19.8 jit_solution(4547647073822263640)
XLA Ops:
  0.0 18.8 %shard_map.46 = bf16[4096,128]{1,0:T(8,128)(2,1)S(1)} custom-call(bf16[4096,128]{1,0:T(8,128)(2,1)} %a_hbm.1, bf16[64,4096]{1,0:T(8,128)(2,1)} %bitcast.2, bf16[256,256]{1,0:T(8,128)(2,1)} %inv_hbm.1, s32[1,256]{1,0:T(1,128)} %bitcast.3), custom_call_target="tpu_custom_call" | custom-call | tf_op jit(solution)/shard_map/pallas_call | solution.py:387
  18.8 1.0 %copy.6 = bf16[4096,128]{1,0:T(8,128)(2,1)} copy(bf16[4096,128]{1,0:T(8,128)(2,1)S(1)} %shard_map.46) | data formatting | bytes 2097152

commit v2 on v1

v2 whole, which is shorter than its diff:
```python
import functools

import jax
import jax.numpy as jnp
from jax import lax
from jax.experimental import pallas as pl
from jax.experimental.pallas import tpu as pltpu
from jax.sharding import PartitionSpec as P

MESH = pl.DeviceIdType.MESH
F32 = jnp.float32
BF16 = jnp.bfloat16
CORES = 2
LOADS = 2
ENTER_AFTER = 0


def one_hot(mask):
    return jnp.where(mask, 1.0, 0.0).astype(BF16)


def column_of(pv_row):
    nb = pv_row.shape[1]
    slot = lax.broadcasted_iota(jnp.int32, (nb, nb), 0)
    other = lax.broadcasted_iota(jnp.int32, (nb, nb), 1)
    return jnp.max(jnp.where(slot == other, pv_row, -1.0), axis=1, keepdims=True)


def swap_plan(pv_row, pv_col):
    nb = pv_row.shape[1]
    slot = lax.broadcasted_iota(jnp.int32, (nb, nb), 0).astype(F32)
    other = lax.broadcasted_iota(jnp.int32, (nb, nb), 1).astype(F32)
    slot_col = lax.broadcasted_iota(jnp.int32, (nb, 1), 0).astype(F32)
    earlier = other < slot
    pointer = jnp.max(jnp.where((pv_row == slot) & earlier, other, -1.0), axis=1, keepdims=True)
    chain = one_hot(other == jnp.where(pointer >= 0, pointer, slot_col))
    for _ in range((nb - 1).bit_length()):
        chain = jnp.dot(chain, chain, preferred_element_type=F32).astype(BF16)
    same = pv_row == pv_col
    previous = jnp.max(jnp.where(same & earlier, other, -1.0), axis=1, keepdims=True)
    via = jnp.dot(one_hot(other == previous), chain, preferred_element_type=F32).astype(BF16)
    repeated = jnp.max(jnp.where(same & (slot > other), 1.0, 0.0), axis=0, keepdims=True)
    landing = jnp.where((repeated < 0.5) & (pv_row >= nb), pv_row, -1.0)
    return previous, via, chain, landing


def kernel(
    n_prow, n_pcol, bounds, tail,
    a_hbm, l_hbm, inv_hbm, pv_hbm, out_v,
    a_v, l_full, inv_v, pv_ref, part, got, mine, tops, origs,
    load_sem, a_sem, send_sem, recv_sem, y_recv, f_recv, flags,
):
    p1_send, p2_send, o1_send, o2_send, y_send, m_send, f_send = (send_sem.at[i] for i in range(7))
    p1_recv, p2_recv, o1_recv, o2_recv, m_recv = (recv_sem.at[i] for i in range(5))
    owner_up, rest_up, mate_in = (flags.at[i] for i in range(3))
    rows, width = a_v.shape
    nb = inv_v.shape[0]
    n_red, piece, _ = part.shape
    depth = l_full.shape[1]
    n_y = n_pcol // CORES
    chunks = len(bounds) - 1
    top = sum(1 for k in range(chunks) if bounds[k + 1] <= nb)
    me = lax.axis_index("prow")
    col = lax.axis_index("pcol")
    y, core = col // CORES, col % CORES
    mate = y * CORES + (1 - core)

    def y_peer(d):
        return lax.rem(y + d, n_y) * CORES + core

    def y_from(d):
        return lax.rem(y + n_y - d, n_y) * CORES + core

    def to(d):
        return lax.rem(me + d, n_prow)

    def frm(d):
        return lax.rem(me + n_prow - d, n_prow)

    def lower(d):
        return me + d >= n_prow

    def is_red(index):
        return index < n_red

    def if_red(index, fn):
        pl.when(is_red(index))(fn)

    slot = lax.rem(me, n_red)

    barrier = pltpu.get_barrier_semaphore()
    for d in range(1, n_y):
        pl.semaphore_signal(barrier, inc=1, device_id=(me, y_peer(d)), device_id_type=MESH)

    @pl.when(core == 1)
    def _():
        pl.semaphore_signal(barrier, inc=1, device_id=(me, mate), device_id_type=MESH)

    for d in range(1, n_prow):
        @pl.when(is_red(me) & jnp.logical_not(lower(d)))
        def _():
            pl.semaphore_signal(barrier, inc=1, device_id=(to(d), y * CORES), device_id_type=MESH)

    pv_load = pltpu.make_async_copy(pv_hbm, pv_ref, load_sem.at[0])
    pv_load.start()
    block = rows // LOADS
    a_loads = [
        pltpu.make_async_copy(
            a_hbm.at[pl.ds(k * block, block)], a_v.at[pl.ds(k * block, block)], a_sem.at[k])
        for k in range(LOADS)
    ]
    for load in a_loads:
        load.start()
    l_load = pltpu.make_async_copy(l_hbm, l_full.at[col], load_sem.at[1])
    inv_load = pltpu.make_async_copy(inv_hbm, inv_v, load_sem.at[0])

    def cols(k):
        return pl.ds(bounds[k], bounds[k + 1] - bounds[k])

    def sent(k, fn):
        if bounds[k + 1] <= nb:
            pl.when(me > 0)(fn)
        else:
            fn()

    def both(chip, k):
        return l_full.at[pl.ds(chip * CORES, CORES), :, cols(k)]

    y_copies = {}
    for k in range(chunks):
        for d in range(1, n_y):
            src, dst = l_hbm.at[:, cols(k)], l_full.at[col, :, cols(k)]
            if k >= tail:
                src = dst = both(y, k)
            y_copies[d, k] = pltpu.make_async_remote_copy(
                src, dst, y_send, y_recv.at[d - 1, k], device_id=(me, y_peer(d)), device_id_type=MESH)
    m_copy = pltpu.make_async_remote_copy(
        l_hbm, l_full.at[col], m_send, m_recv, device_id=(me, mate), device_id_type=MESH)

    def enter():
        pl.semaphore_wait(
            barrier, n_y - 1 + jnp.where(core == 0, 1 + CORES * jnp.minimum(me, n_red), 0))
        for k in range(tail):
            for d in range(1, n_y):
                sent(k, y_copies[d, k].start)
        @pl.when(core == 0)
        def _():
            pl.semaphore_signal(mate_in, inc=1, device_id=(me, mate), device_id_type=MESH)
            m_copy.start()
            for d in range(1, n_prow):
                for c in range(CORES):
                    there = (to(d), y * CORES + c)

                    @pl.when(is_red(me) & lower(d))
                    def _():
                        pl.semaphore_signal(owner_up, inc=1, device_id=there, device_id_type=MESH)

                    @pl.when(jnp.logical_not(is_red(me)) & is_red(to(d)))
                    def _():
                        pl.semaphore_signal(rest_up, inc=1, device_id=there, device_id_type=MESH)

    at_once = (core == 1) | (me == 0)
    pl.when(at_once)(enter)
    l_load.start()

    def global_rows(shape, axis, start):
        local = lax.broadcasted_iota(jnp.int32, shape, axis) + start
        return ((local // nb * n_prow + me) * nb + local % nb).astype(F32)

    pv_load.wait()
    inv_load.start()
    pv_row = pv_ref[...].astype(F32)
    pv_col = column_of(pv_row)
    total = jnp.zeros((nb, width), F32)
    for k in range(LOADS):
        a_loads[k].wait()
        pick = one_hot(pv_col == global_rows((1, block), 1, k * block))
        total = total + jnp.dot(pick, a_v[pl.ds(k * block, block), :], preferred_element_type=F32)
        if k == ENTER_AFTER:
            pl.when(jnp.logical_not(at_once))(enter)
    part[...] = total.astype(BF16).reshape(n_red, piece, width)

    @pl.when(core == 1)
    def _():
        pl.semaphore_wait(mate_in, 1)
        m_copy.start()

    p1_copies = {}
    for d in range(1, n_prow):
        t = to(d)
        p1_copies[d] = pltpu.make_async_remote_copy(
            part.at[lax.rem(t, n_red)], got.at[d], p1_send, p1_recv,
            device_id=(t, col), device_id_type=MESH)
        pl.when(is_red(t) & lower(d))(p1_copies[d].start)

    inv_load.wait()
    pv_row = pv_ref[...].astype(F32)
    previous, via, chain, landing = swap_plan(pv_row, column_of(pv_row))

    @pl.when(me < n_red - 1)
    def _():
        pl.semaphore_wait(owner_up, n_red - 1 - me)

    o1_copies = [
        pltpu.make_async_remote_copy(
            a_v.at[pl.ds(t * piece, piece)], origs.at[pl.ds(t * piece, piece)], o1_send, o1_recv,
            device_id=(t, col), device_id_type=MESH)
        for t in range(1, n_red)
    ]
    o_local = pltpu.make_async_copy(a_v.at[pl.ds(0, nb)], origs, o1_recv)

    @pl.when(me == 0)
    def _():
        o_local.start()
        for copy in o1_copies:
            copy.start()

    for d in range(1, n_prow):
        pl.when(is_red(to(d)) & jnp.logical_not(lower(d)))(p1_copies[d].start)

    m_copy.wait_recv()
    l_load.wait()

    @pl.when(core == 1)
    def _():
        for k in range(tail, chunks):
            for d in range(1, n_y):
                y_copies[d, k].start()

    f_copies = {}
    for k in range(chunks):
        for d in range(1, n_y):
            src = l_full.at[y_from(d), :, cols(k)]
            if k >= tail:
                src = both(y_from(d) // CORES, k)
            f_copies[d, k] = pltpu.make_async_remote_copy(
                src, src, f_send, f_recv.at[d - 1, k], device_id=(me, mate), device_id_type=MESH)

    def forward(k):
        if k >= chunks:
            return

        def go():
            for d in range(1, n_y):
                y_copies[d, k].wait_recv()
                f_copies[d, k].start()

        if k >= tail:
            pl.when(core == 1)(go)
        else:
            sent(k, go)

    own_rows = origs.at[pl.ds(slot * piece, piece)]
    o2_copies, p2_copies = {}, {}
    for d in range(1, n_prow):
        o2_copies[d] = pltpu.make_async_remote_copy(
            own_rows, own_rows, o2_send, o2_recv,
            device_id=(to(d), col), device_id_type=MESH)
        p2_copies[d] = pltpu.make_async_remote_copy(
            mine, tops.at[pl.ds(slot * piece, piece)], p2_send, p2_recv,
            device_id=(to(d), col), device_id_type=MESH)

    def not_first(d, fn):
        pl.when(me + d != n_prow)(fn)

    def send_orig():
        @pl.when(me == 0)
        def _():
            o_local.wait()

        @pl.when(me > 0)
        def _():
            pltpu.make_async_remote_copy(
                a_v.at[pl.ds(0, piece)], own_rows, o1_send, o1_recv,
                device_id=(0, col), device_id_type=MESH).wait_recv()

        pl.semaphore_wait(rest_up, n_prow - n_red)
        for d in range(1, n_prow):
            not_first(d, o2_copies[d].start)

    def arrive(ref, sem):
        pltpu.make_async_copy(ref, ref, sem).wait()

    def gather(ref, sem):
        if_red(me, lambda: arrive(ref.at[pl.ds(0, nb - piece)], sem))
        pl.when(jnp.logical_not(is_red(me)))(lambda: arrive(ref, sem))

    if_red(me, send_orig)
    forward(0)
    forward(1)

    def reduce_and_send():
        acc = part[slot].astype(F32)
        arrive(got.at[pl.ds(1, n_prow - 1)], p1_recv)
        for d in range(1, n_prow):
            acc = acc + got[d].astype(F32)
        mine[...] = acc.astype(BF16)
        tops[pl.ds(slot * piece, piece), :] = acc.astype(BF16)
        for d in range(1, n_prow):
            p2_copies[d].start()

    if_red(me, reduce_and_send)
    forward(2)

    late = [tail - 1] if tail - 1 > 2 else []
    far = (core == 1) | (me >= n_prow * 3 // 4)
    for k in late:
        pl.when(far)(functools.partial(forward, k))

    pl.when(me > 0)(lambda: gather(origs, o2_recv))
    orig = origs[...]
    moved = jnp.dot(chain, orig, preferred_element_type=F32).astype(BF16)
    again = jnp.dot(via, orig, preferred_element_type=F32).astype(BF16)
    moved = jnp.concatenate([moved, jnp.ones((nb, width), BF16)], axis=1)
    step = min(512, rows)
    for start in range(0, rows, step):
        here = one_hot(landing == global_rows((step, 1), 0, start))
        both = jnp.dot(here, moved, preferred_element_type=F32)
        rows_k = pl.ds(start, step)
        out_v[rows_k, :] = jnp.where(
            both[:, width:] > 0.5, both[:, :width], a_v[rows_k, :].astype(F32)).astype(BF16)

    for k in late:
        pl.when(jnp.logical_not(far))(functools.partial(forward, k))
    forward(tail)
    gather(tops, p2_recv)
    top_rows = jnp.where(previous >= 0, again, tops[...])
    u_block = jnp.dot(inv_v[...], top_rows, preferred_element_type=F32).astype(BF16)

    def arrived(k):
        def go():
            for d in range(1, n_y):
                f_copies[d, k].wait_recv()
        if k >= tail:
            pl.when(core == 0)(go)
        else:
            sent(k, go)

    def update(first, last):
        for k in range(first, last):
            arrived(k)
        start, stop = bounds[first], bounds[last]
        rows_k = pl.ds(start, stop - start)
        panel = l_full[:, :, rows_k].reshape(nb, stop - start)
        product = lax.dot_general(
            panel, u_block, (((0,), (0,)), ((), ())), preferred_element_type=F32)
        out_v[rows_k, :] = (out_v[rows_k, :].astype(F32) - product).astype(BF16)

    most = max(top, tail - 1)

    @pl.when(me > 0)
    def _():
        update(0, most)

    @pl.when(me == 0)
    def _():
        out_v[pl.ds(0, bounds[top]), :] = u_block[:bounds[top], :]
        if most > top:
            update(top, most)

    for k in range(tail + 1, chunks):
        forward(k)
    if min(tail + 1, chunks) > most:
        update(most, min(tail + 1, chunks))
    if chunks > tail + 1:
        update(tail + 1, chunks)

    @pl.when(me == 0)
    def _():
        arrive(origs.at[pl.ds(0, nb - piece)], o1_send)

    m_copy.wait_send()
    if_red(me, lambda: arrive(part.at[pl.ds(0, n_red - 1)], p1_send))
    pl.when(jnp.logical_not(is_red(me)))(lambda: arrive(part, p1_send))

    def drain():
        @pl.when(me == 0)
        def _():
            arrive(got.at[pl.ds(1, n_prow - 1)], o2_send)

        @pl.when(me > 0)
        def _():
            arrive(got.at[pl.ds(1, n_prow - 2)], o2_send)

        arrive(got.at[pl.ds(1, n_prow - 1)], p2_send)

    if_red(me, drain)

    def sent_all(lanes):
        tiles = lanes * (n_y - 1) // 128
        if tiles:
            full = rows // 128
            count = next((n for n in range(1, n_pcol + 1) if tiles % n == 0 and tiles // n <= full), 0)
            parts = [(count, tiles // count)] if count else [(tiles // full, full), (1, tiles % full)]
            for count, wide in parts:
                whole = l_full.at[pl.ds(0, count), :, pl.ds(0, wide * 128)]
                arrive(whole, y_send)
                arrive(whole, f_send)

    for skip, here in ((0, me > 0), (bounds[top], me == 0)):
        pl.when(here & (core == 0))(functools.partial(sent_all, bounds[tail] - skip))
        pl.when(here & (core == 1))(functools.partial(sent_all, 2 * rows - bounds[tail] - skip))


def hbm(array):
    return pltpu.with_memory_space_constraint(array, pltpu.HBM)


def chunk_bounds(rows, nb):
    last = min(5 * nb, (rows - nb) // 2)
    bounds = [0, nb]
    while bounds[-1] < rows - last:
        bounds.append(min(bounds[-1] + 4 * nb, rows - last))
    tail = len(bounds) - 1
    if last == 5 * nb:
        bounds += [rows - 5 * nb // 2, rows - nb]
    return (*bounds, rows), tail


def body(n_prow, n_pcol, a_matrix, l_panel, l_inverse, pivots):
    rows, width = a_matrix.shape
    nb = l_inverse.shape[0]
    depth = l_panel.shape[1]
    n_red = min(n_prow // 2, nb // 16)
    piece = nb // n_red
    n_y = n_pcol // CORES
    bounds, tail = chunk_bounds(rows, nb)
    chunks = len(bounds) - 1
    dma = pltpu.SemaphoreType.DMA
    flag = pltpu.SemaphoreType.REGULAR
    return pl.pallas_call(
        functools.partial(kernel, n_prow, n_pcol, bounds, tail),
        out_shape=jax.ShapeDtypeStruct((rows, width), BF16),
        in_specs=[pl.BlockSpec(memory_space=pl.ANY)] * 4,
        out_specs=pl.BlockSpec(memory_space=pltpu.VMEM),
        scratch_shapes=[
            pltpu.VMEM((rows, width), BF16),
            pltpu.VMEM((n_pcol, depth, rows), BF16),
            pltpu.VMEM((nb, nb), BF16),
            pltpu.VMEM((1, nb), jnp.int32),
            pltpu.VMEM((n_red, piece, width), BF16),
            pltpu.VMEM((n_prow, piece, width), BF16),
            pltpu.VMEM((piece, width), BF16),
            pltpu.VMEM((nb, width), BF16),
            pltpu.VMEM((nb, width), BF16),
            dma((2,)), dma((LOADS,)), dma((7,)), dma((5,)),
            dma((max(n_y - 1, 1), chunks)), dma((max(n_y - 1, 1), chunks)), flag((3,)),
        ],
        compiler_params=pltpu.CompilerParams(
            collective_id=0, has_side_effects=True, vmem_limit_bytes=24 * 2 ** 20),
    )(hbm(a_matrix), hbm(l_panel.T), hbm(l_inverse), hbm(pivots.reshape(1, nb)))


def solution(mesh):
    n_prow, n_pcol = mesh.shape["prow"], mesh.shape["pcol"]
    in_specs = (P("prow", "pcol"), P("prow", "pcol"), P(), P())
    return jax.shard_map(
        functools.partial(body, n_prow, n_pcol),
        mesh=mesh, in_specs=in_specs, out_specs=P("prow", "pcol"), check_vma=False)
```

time: 19.9 us -> 16.8 us (0.84)
  the two profiles are of different devices: /device:TPU:27 before, /device:TPU:0 now
where the time goes in v2:
time: 16.8 us; the launch traced here: 16.6 us
  Pallas kernels  15.7 us (93%)
  local copies, waits for them, and re-layouts  0.97 us (6%)
    pallas_call x1, Pallas kernels, body(): pl.pallas_call(functools.partial(kernel, n_prow, n_pcol, bounds, tail), o...  15.7 us
    unnamed x1, local copies, waits for them, and re-layouts  0.97 us

profile of v2, /device:TPU:0, one launch (start us, length us, event | category | flops | bytes accessed | tf_op | source)
XLA Modules:
  0.0 16.6 jit_solution(11235811190364975969)
XLA Ops:
  0.0 15.7 %shard_map.46 = bf16[4096,128]{1,0:T(8,128)(2,1)S(1)} custom-call(bf16[4096,128]{1,0:T(8,128)(2,1)} %a_hbm.1, bf16[64,4096]{1,0:T(8,128)(2,1)} %bitcast.2, bf16[256,256]{1,0:T(8,128)(2,1)} %inv_hbm.1, s32[1,256]{1,0:T(1,128)} %bitcast.3), custom_call_target="tpu_custom_call" | custom-call | tf_op jit(solution)/shard_map/pallas_call | solution.py:431
  15.7 1.0 %copy.6 = bf16[4096,128]{1,0:T(8,128)(2,1)} copy(bf16[4096,128]{1,0:T(8,128)(2,1)S(1)} %shard_map.46) | data formatting | bytes 2097152

commit v3 on v2

--- a/solution.py
+++ b/solution.py
@@ -46,8 +46,8 @@
 
 def kernel(
     n_prow, n_pcol, bounds, tail,
-    a_hbm, l_hbm, inv_hbm, pv_hbm, out_v,
-    a_v, l_full, inv_v, pv_ref, part, got, mine, tops, origs,
+    a_hbm, l_hbm, inv_hbm, pv_hbm, out_v, l_full, u_out,
+    a_v, here_v, inv_v, pv_ref, part, got, mine, tops, origs,
     load_sem, a_sem, send_sem, recv_sem, y_recv, f_recv, flags,
 ):
     p1_send, p2_send, o1_send, o2_send, y_send, m_send, f_send = (send_sem.at[i] for i in range(7))
@@ -96,11 +96,6 @@
     def _():
         pl.semaphore_signal(barrier, inc=1, device_id=(me, mate), device_id_type=MESH)
 
-    for d in range(1, n_prow):
-        @pl.when(is_red(me) & jnp.logical_not(lower(d)))
-        def _():
-            pl.semaphore_signal(barrier, inc=1, device_id=(to(d), y * CORES), device_id_type=MESH)
-
     pv_load = pltpu.make_async_copy(pv_hbm, pv_ref, load_sem.at[0])
     pv_load.start()
     block = rows // LOADS
@@ -111,6 +106,11 @@
     ]
     for load in a_loads:
         load.start()
+    for d in range(1, n_prow):
+        @pl.when(is_red(me) & jnp.logical_not(lower(d)))
+        def _():
+            pl.semaphore_signal(barrier, inc=1, device_id=(to(d), y * CORES), device_id_type=MESH)
+
     l_load = pltpu.make_async_copy(l_hbm, l_full.at[col], load_sem.at[1])
     inv_load = pltpu.make_async_copy(inv_hbm, inv_v, load_sem.at[0])
 
@@ -134,6 +134,13 @@
                 src = dst = both(y, k)
             y_copies[d, k] = pltpu.make_async_remote_copy(
                 src, dst, y_send, y_recv.at[d - 1, k], device_id=(me, y_peer(d)), device_id_type=MESH)
+    last = chunks - 1
+    y_twice = [
+        pltpu.make_async_remote_copy(
+            both(y, last), both(y, last), y_send, y_recv.at[d - 1, last],
+            device_id=(me, y_peer(d) - core), device_id_type=MESH)
+        for d in range(1, n_y)
+    ]
     m_copy = pltpu.make_async_remote_copy(
         l_hbm, l_full.at[col], m_send, m_recv, device_id=(me, mate), device_id_type=MESH)
 
@@ -225,6 +232,8 @@
     def _():
         for k in range(tail, chunks):
             for d in range(1, n_y):
+                if k == last:
+                    y_twice[d - 1].start()
                 y_copies[d, k].start()
 
     f_copies = {}
@@ -245,7 +254,10 @@
                 y_copies[d, k].wait_recv()
                 f_copies[d, k].start()
 
-        if k >= tail:
+        if k == last:
+            for d in range(1, n_y):
+                y_copies[d, k].wait_recv()
+        elif k >= tail:
             pl.when(core == 1)(go)
         else:
             sent(k, go)
@@ -286,8 +298,15 @@
         pl.when(jnp.logical_not(is_red(me)))(lambda: arrive(ref, sem))
 
     if_red(me, send_orig)
+    step = min(512, rows)
+    for start in range(0, rows, step):
+        rows_k = pl.ds(start, step)
+        here = one_hot(landing == global_rows((step, 1), 0, start))
+        here_v[rows_k, :] = here
+        hit = jnp.dot(here, jnp.ones((nb, width), BF16), preferred_element_type=F32)
+        out_v[rows_k, :] = jnp.where(hit > 0.5, 0.0, a_v[rows_k, :].astype(F32)).astype(BF16)
+
     forward(0)
-    forward(1)
 
     def reduce_and_send():
         acc = part[slot].astype(F32)
@@ -297,9 +316,12 @@
         mine[...] = acc.astype(BF16)
         tops[pl.ds(slot * piece, piece), :] = acc.astype(BF16)
         for d in range(1, n_prow):
-            p2_copies[d].start()
+            pl.when(me + d == n_prow)(p2_copies[d].start)
+        for d in range(1, n_prow):
+            not_first(d, p2_copies[d].start)
 
     if_red(me, reduce_and_send)
+    forward(1)
     forward(2)
 
     late = [tail - 1] if tail - 1 > 2 else []
@@ -311,18 +333,15 @@
     orig = origs[...]
     moved = jnp.dot(chain, orig, preferred_element_type=F32).astype(BF16)
     again = jnp.dot(via, orig, preferred_element_type=F32).astype(BF16)
-    moved = jnp.concatenate([moved, jnp.ones((nb, width), BF16)], axis=1)
-    step = min(512, rows)
     for start in range(0, rows, step):
-        here = one_hot(landing == global_rows((step, 1), 0, start))
-        both = jnp.dot(here, moved, preferred_element_type=F32)
         rows_k = pl.ds(start, step)
-        out_v[rows_k, :] = jnp.where(
-            both[:, width:] > 0.5, both[:, :width], a_v[rows_k, :].astype(F32)).astype(BF16)
+        landed = jnp.dot(here_v[rows_k, :], moved, preferred_element_type=F32)
+        out_v[rows_k, :] = (out_v[rows_k, :].astype(F32) + landed).astype(BF16)
 
     for k in late:
         pl.when(jnp.logical_not(far))(functools.partial(forward, k))
-    forward(tail)
+    if tail < last:
+        forward(tail)
     gather(tops, p2_recv)
     top_rows = jnp.where(previous >= 0, again, tops[...])
     u_block = jnp.dot(inv_v[...], top_rows, preferred_element_type=F32).astype(BF16)
@@ -331,9 +350,9 @@
         def go():
             for d in range(1, n_y):
                 f_copies[d, k].wait_recv()
-        if k >= tail:
+        if last > k >= tail:
             pl.when(core == 0)(go)
-        else:
+        elif k < tail:
             sent(k, go)
 
     def update(first, last):
@@ -358,12 +377,15 @@
         if most > top:
             update(top, most)
 
-    for k in range(tail + 1, chunks):
+    u_out[...] = u_block
+    for k in range(tail + 1, last):
         forward(k)
-    if min(tail + 1, chunks) > most:
-        update(most, min(tail + 1, chunks))
-    if chunks > tail + 1:
-        update(tail + 1, chunks)
+    split = min(tail + 1, last)
+    if split > most:
+        update(most, split)
+    for k in range(split, last):
+        arrived(k)
+    forward(last)
 
     @pl.when(me == 0)
     def _():
@@ -386,20 +408,38 @@
 
     if_red(me, drain)
 
-    def sent_all(lanes):
+    def sent_all(lanes, sem):
         tiles = lanes * (n_y - 1) // 128
         if tiles:
             full = rows // 128
             count = next((n for n in range(1, n_pcol + 1) if tiles % n == 0 and tiles // n <= full), 0)
             parts = [(count, tiles // count)] if count else [(tiles // full, full), (1, tiles % full)]
             for count, wide in parts:
-                whole = l_full.at[pl.ds(0, count), :, pl.ds(0, wide * 128)]
-                arrive(whole, y_send)
-                arrive(whole, f_send)
-
+                arrive(l_full.at[pl.ds(0, count), :, pl.ds(0, wide * 128)], sem)
+
+    shared, end = rows - bounds[tail], rows - bounds[last]
     for skip, here in ((0, me > 0), (bounds[top], me == 0)):
-        pl.when(here & (core == 0))(functools.partial(sent_all, bounds[tail] - skip))
-        pl.when(here & (core == 1))(functools.partial(sent_all, 2 * rows - bounds[tail] - skip))
+        @pl.when(here & (core == 0))
+        def _():
+            sent_all(bounds[tail] - skip, y_send)
+            sent_all(bounds[tail] - skip, f_send)
+
+        @pl.when(here & (core == 1))
+        def _():
+            sent_all(rows + shared + 2 * end - skip, y_send)
+            sent_all(rows + shared - 2 * end - skip, f_send)
+
+
+def last_update(start, in_v, l_full, u_in, out_hbm, end_v, sem):
+    rows, width = in_v.shape
+    nb = u_in.shape[0]
+    rows_k = pl.ds(start, rows - start)
+    pltpu.make_async_copy(in_v.at[pl.ds(0, start)], out_hbm.at[pl.ds(0, start)], sem).start()
+    panel = l_full[:, :, rows_k].reshape(nb, rows - start)
+    product = lax.dot_general(panel, u_in[...], (((0,), (0,)), ((), ())), preferred_element_type=F32)
+    end_v[...] = (in_v[rows_k, :].astype(F32) - product).astype(BF16)
+    pltpu.make_async_copy(end_v, out_hbm.at[rows_k], sem).start()
+    pltpu.make_async_copy(in_v, out_hbm, sem).wait()
 
 
 def hbm(array):
@@ -413,7 +453,7 @@
         bounds.append(min(bounds[-1] + 4 * nb, rows - last))
     tail = len(bounds) - 1
     if last == 5 * nb:
-        bounds += [rows - 5 * nb // 2, rows - nb]
+        bounds += [rows - 2 * nb, rows - nb // 2]
     return (*bounds, rows), tail
 
 
@@ -428,14 +468,18 @@
     chunks = len(bounds) - 1
     dma = pltpu.SemaphoreType.DMA
     flag = pltpu.SemaphoreType.REGULAR
-    return pl.pallas_call(
+    most_rows, l_all, u_block = pl.pallas_call(
         functools.partial(kernel, n_prow, n_pcol, bounds, tail),
-        out_shape=jax.ShapeDtypeStruct((rows, width), BF16),
+        out_shape=[
+            jax.ShapeDtypeStruct((rows, width), BF16),
+            jax.ShapeDtypeStruct((n_pcol, depth, rows), BF16),
+            jax.ShapeDtypeStruct((nb, width), BF16),
+        ],
         in_specs=[pl.BlockSpec(memory_space=pl.ANY)] * 4,
-        out_specs=pl.BlockSpec(memory_space=pltpu.VMEM),
+        out_specs=[pl.BlockSpec(memory_space=pltpu.VMEM)] * 3,
         scratch_shapes=[
             pltpu.VMEM((rows, width), BF16),
-            pltpu.VMEM((n_pcol, depth, rows), BF16),
+            pltpu.VMEM((rows, nb), BF16),
             pltpu.VMEM((nb, nb), BF16),
             pltpu.VMEM((1, nb), jnp.int32),
             pltpu.VMEM((n_red, piece, width), BF16),
@@ -449,6 +493,15 @@
         compiler_params=pltpu.CompilerParams(
             collective_id=0, has_side_effects=True, vmem_limit_bytes=24 * 2 ** 20),
     )(hbm(a_matrix), hbm(l_panel.T), hbm(l_inverse), hbm(pivots.reshape(1, nb)))
+    start = bounds[min(tail + 1, chunks - 1)]
+    return pl.pallas_call(
+        functools.partial(last_update, start),
+        out_shape=jax.ShapeDtypeStruct((rows, width), BF16),
+        in_specs=[pl.BlockSpec(memory_space=pltpu.VMEM)] * 3,
+        out_specs=pl.BlockSpec(memory_space=pltpu.HBM),
+        scratch_shapes=[pltpu.VMEM((rows - start, width), BF16), dma],
+        compiler_params=pltpu.CompilerParams(vmem_limit_bytes=8 * 2 ** 20),
+    )(most_rows, l_all, u_block)
 
 
 def solution(mesh):

time: 16.8 us -> 16.3 us (0.970)
  local copies, waits for them, and re-layouts: 0.97 us -> 0 us
  Pallas kernels: 15.7 us -> 16.2 us
    unnamed x1 -> x0, local copies, waits for them, and re-layouts: 0.97 us -> none
    pallas_call x0 -> x1, Pallas kernels: none -> 0.97 us  [body(): pl.pallas_call(functools.partial(last_update, start), out_shape=jax.Shape...]
    pallas_call x1, Pallas kernels: 15.7 us -> 15.2 us  [body(): pl.pallas_call(functools.partial(kernel, n_prow, n_pcol, bounds, tail), o...]
where the time goes in v3:
time: 16.3 us; the launch traced here: 16.2 us
  Pallas kernels  16.2 us (99%)
    pallas_call x1, Pallas kernels, body(): pl.pallas_call(functools.partial(kernel, n_prow, n_pcol, bounds, tail), o...  15.2 us
    pallas_call x1, Pallas kernels, body(): pl.pallas_call(functools.partial(last_update, start), out_shape=jax.Shape...  0.97 us

profile of v3, /device:TPU:0, one launch (start us, length us, event | category | flops | bytes accessed | tf_op | source)
XLA Modules:
  0.0 16.2 jit_solution(13770259580893378711)
XLA Ops:
  0.0 15.2 %shard_map.46 = (bf16[4096,128]{1,0:T(8,128)(2,1)S(1)}, bf16[4,64,4096]{2,1,0:T(8,128)(2,1)S(1)}, bf16[256,128]{1,0:T(8,128)(2,1)S(1)}) custom-call(bf16[4096,128]{1,0:T(8,128)(2,1)} %a_hbm.1, bf16[64,4096]{1,0:T(8,128)(2,1)} %bitcast.2, bf16[256,256]{1,0:T(8,128)(2,1)} %inv_hbm.1, s32[1,256]{1,0:T(1,128)} %bitcast.3), custom_call_target="tpu_custom_call" | custom-call | tf_op jit(solution)/shard_map/pallas_call | solution.py:471
  15.2 1.0 %shard_map.47 = bf16[4096,128]{1,0:T(8,128)(2,1)} custom-call(bf16[4096,128]{1,0:T(8,128)(2,1)S(1)} %get-tuple-element.8.in_v, bf16[4,64,4096]{2,1,0:T(8,128)(2,1)S(1)} %get-tuple-element.9.l_full, bf16[256,128]{1,0:T(8,128)(2,1)S(1)} %get-tuple-element.10.u_in), custom_call_target="tpu_custom_call" | custom-call | tf_op jit(solution)/shard_map/pallas_call | solution.py:497

commit v4 on v3

--- a/solution.py
+++ b/solution.py
@@ -193,7 +193,7 @@
         m_copy.start()
 
     p1_copies = {}
-    for d in range(1, n_prow):
+    for d in reversed(range(1, n_prow)):
         t = to(d)
         p1_copies[d] = pltpu.make_async_remote_copy(
             part.at[lax.rem(t, n_red)], got.at[d], p1_send, p1_recv,

time: 16.3 us -> 16.3 us (level)
  no operation moved by 1% of the time
where the time goes in v4:
time: 16.3 us; the launch traced here: 16.2 us
  Pallas kernels  16.2 us (99%)
    pallas_call x1, Pallas kernels, body(): pl.pallas_call(functools.partial(kernel, n_prow, n_pcol, bounds, tail), o...  15.2 us
    pallas_call x1, Pallas kernels, body(): pl.pallas_call(functools.partial(last_update, start), out_shape=jax.Shape...  0.97 us

profile of v4, /device:TPU:0, one launch (start us, length us, event | category | flops | bytes accessed | tf_op | source)
XLA Modules:
  0.0 16.2 jit_solution(9321354770171668394)
XLA Ops:
  0.0 15.2 %shard_map.46 = (bf16[4096,128]{1,0:T(8,128)(2,1)S(1)}, bf16[4,64,4096]{2,1,0:T(8,128)(2,1)S(1)}, bf16[256,128]{1,0:T(8,128)(2,1)S(1)}) custom-call(bf16[4096,128]{1,0:T(8,128)(2,1)} %a_hbm.1, bf16[64,4096]{1,0:T(8,128)(2,1)} %bitcast.2, bf16[256,256]{1,0:T(8,128)(2,1)} %inv_hbm.1, s32[1,256]{1,0:T(1,128)} %bitcast.3), custom_call_target="tpu_custom_call" | custom-call | tf_op jit(solution)/shard_map/pallas_call | solution.py:471
  15.2 1.0 %shard_map.47 = bf16[4096,128]{1,0:T(8,128)(2,1)} custom-call(bf16[4096,128]{1,0:T(8,128)(2,1)S(1)} %get-tuple-element.8.in_v, bf16[4,64,4096]{2,1,0:T(8,128)(2,1)S(1)} %get-tuple-element.9.l_full, bf16[256,128]{1,0:T(8,128)(2,1)S(1)} %get-tuple-element.10.u_in), custom_call_target="tpu_custom_call" | custom-call | tf_op jit(solution)/shard_map/pallas_call | solution.py:497

commit v5 on v4

--- a/solution.py
+++ b/solution.py
@@ -298,16 +298,6 @@
         pl.when(jnp.logical_not(is_red(me)))(lambda: arrive(ref, sem))
 
     if_red(me, send_orig)
-    step = min(512, rows)
-    for start in range(0, rows, step):
-        rows_k = pl.ds(start, step)
-        here = one_hot(landing == global_rows((step, 1), 0, start))
-        here_v[rows_k, :] = here
-        hit = jnp.dot(here, jnp.ones((nb, width), BF16), preferred_element_type=F32)
-        out_v[rows_k, :] = jnp.where(hit > 0.5, 0.0, a_v[rows_k, :].astype(F32)).astype(BF16)
-
-    forward(0)
-
     def reduce_and_send():
         acc = part[slot].astype(F32)
         arrive(got.at[pl.ds(1, n_prow - 1)], p1_recv)
@@ -320,7 +310,19 @@
         for d in range(1, n_prow):
             not_first(d, p2_copies[d].start)
 
-    if_red(me, reduce_and_send)
+    pl.when((me > 0) & is_red(me))(reduce_and_send)
+
+    step = min(512, rows)
+    for start in range(0, rows, step):
+        rows_k = pl.ds(start, step)
+        here = one_hot(landing == global_rows((step, 1), 0, start))
+        here_v[rows_k, :] = here
+        hit = jnp.dot(here, jnp.ones((nb, width), BF16), preferred_element_type=F32)
+        out_v[rows_k, :] = jnp.where(hit > 0.5, 0.0, a_v[rows_k, :].astype(F32)).astype(BF16)
+
+    forward(0)
+
+    pl.when(me == 0)(reduce_and_send)
     forward(1)
     forward(2)
 

time: 16.3 us -> 16.2 us (level)
  Pallas kernels: 16.2 us -> 16 us
    pallas_call x1, Pallas kernels: 15.2 us -> 15 us  [body(): pl.pallas_call(functools.partial(kernel, n_prow, n_pcol, bounds, tail), o...]
where the time goes in v5:
time: 16.2 us; the launch traced here: 16 us
  Pallas kernels  16 us (99%)
    pallas_call x1, Pallas kernels, body(): pl.pallas_call(functools.partial(kernel, n_prow, n_pcol, bounds, tail), o...  15 us
    pallas_call x1, Pallas kernels, body(): pl.pallas_call(functools.partial(last_update, start), out_shape=jax.Shape...  0.97 us

profile of v5, /device:TPU:0, one launch (start us, length us, event | category | flops | bytes accessed | tf_op | source)
XLA Modules:
  0.0 16.0 jit_solution(8995201851210342057)
XLA Ops:
  0.0 15.0 %shard_map.46 = (bf16[4096,128]{1,0:T(8,128)(2,1)S(1)}, bf16[4,64,4096]{2,1,0:T(8,128)(2,1)S(1)}, bf16[256,128]{1,0:T(8,128)(2,1)S(1)}) custom-call(bf16[4096,128]{1,0:T(8,128)(2,1)} %a_hbm.1, bf16[64,4096]{1,0:T(8,128)(2,1)} %bitcast.2, bf16[256,256]{1,0:T(8,128)(2,1)} %inv_hbm.1, s32[1,256]{1,0:T(1,128)} %bitcast.3), custom_call_target="tpu_custom_call" | custom-call | tf_op jit(solution)/shard_map/pallas_call | solution.py:473
  15.0 1.0 %shard_map.47 = bf16[4096,128]{1,0:T(8,128)(2,1)} custom-call(bf16[4096,128]{1,0:T(8,128)(2,1)S(1)} %get-tuple-element.8.in_v, bf16[4,64,4096]{2,1,0:T(8,128)(2,1)S(1)} %get-tuple-element.9.l_full, bf16[256,128]{1,0:T(8,128)(2,1)S(1)} %get-tuple-element.10.u_in), custom_call_target="tpu_custom_call" | custom-call | tf_op jit(solution)/shard_map/pallas_call | solution.py:499

commit v6 on v5

--- a/solution.py
+++ b/solution.py
@@ -50,7 +50,8 @@
     a_v, here_v, inv_v, pv_ref, part, got, mine, tops, origs,
     load_sem, a_sem, send_sem, recv_sem, y_recv, f_recv, flags,
 ):
-    p1_send, p2_send, o1_send, o2_send, y_send, m_send, f_send = (send_sem.at[i] for i in range(7))
+    p1_send = p2_send = o1_send = o2_send = send_sem.at[0]
+    y_send = m_send = f_send = send_sem.at[1]
     p1_recv, p2_recv, o1_recv, o2_recv, m_recv = (recv_sem.at[i] for i in range(5))
     owner_up, rest_up, mate_in = (flags.at[i] for i in range(3))
     rows, width = a_v.shape
@@ -59,7 +60,6 @@
     depth = l_full.shape[1]
     n_y = n_pcol // CORES
     chunks = len(bounds) - 1
-    top = sum(1 for k in range(chunks) if bounds[k + 1] <= nb)
     me = lax.axis_index("prow")
     col = lax.axis_index("pcol")
     y, core = col // CORES, col % CORES
@@ -118,22 +118,22 @@
         return pl.ds(bounds[k], bounds[k + 1] - bounds[k])
 
     def sent(k, fn):
-        if bounds[k + 1] <= nb:
-            pl.when(me > 0)(fn)
+        if k == 0:
+            pl.when(me > 0)(lambda: fn(cols(k)))
+            pl.when(me == 0)(lambda: fn(pl.ds(nb, bounds[1] - nb)))
         else:
-            fn()
+            fn(cols(k))
 
     def both(chip, k):
         return l_full.at[pl.ds(chip * CORES, CORES), :, cols(k)]
 
-    y_copies = {}
-    for k in range(chunks):
-        for d in range(1, n_y):
-            src, dst = l_hbm.at[:, cols(k)], l_full.at[col, :, cols(k)]
-            if k >= tail:
-                src = dst = both(y, k)
-            y_copies[d, k] = pltpu.make_async_remote_copy(
-                src, dst, y_send, y_recv.at[d - 1, k], device_id=(me, y_peer(d)), device_id_type=MESH)
+    def y_copy(d, k, at):
+        src, dst = l_hbm.at[:, at], l_full.at[col, :, at]
+        if k >= tail:
+            src = dst = both(y, k)
+        return pltpu.make_async_remote_copy(
+            src, dst, y_send, y_recv.at[d - 1, k], device_id=(me, y_peer(d)), device_id_type=MESH)
+
     last = chunks - 1
     y_twice = [
         pltpu.make_async_remote_copy(
@@ -149,7 +149,7 @@
             barrier, n_y - 1 + jnp.where(core == 0, 1 + CORES * jnp.minimum(me, n_red), 0))
         for k in range(tail):
             for d in range(1, n_y):
-                sent(k, y_copies[d, k].start)
+                sent(k, lambda at: y_copy(d, k, at).start())
         @pl.when(core == 0)
         def _():
             pl.semaphore_signal(mate_in, inc=1, device_id=(me, mate), device_id_type=MESH)
@@ -234,31 +234,27 @@
             for d in range(1, n_y):
                 if k == last:
                     y_twice[d - 1].start()
-                y_copies[d, k].start()
-
-    f_copies = {}
-    for k in range(chunks):
-        for d in range(1, n_y):
-            src = l_full.at[y_from(d), :, cols(k)]
-            if k >= tail:
-                src = both(y_from(d) // CORES, k)
-            f_copies[d, k] = pltpu.make_async_remote_copy(
-                src, src, f_send, f_recv.at[d - 1, k], device_id=(me, mate), device_id_type=MESH)
+                y_copy(d, k, cols(k)).start()
+
+    def f_copy(d, k, at):
+        src = l_full.at[y_from(d), :, at]
+        if k >= tail:
+            src = both(y_from(d) // CORES, k)
+        return pltpu.make_async_remote_copy(
+            src, src, f_send, f_recv.at[d - 1, k], device_id=(me, mate), device_id_type=MESH)
 
     def forward(k):
         if k >= chunks:
             return
 
-        def go():
+        def go(at):
             for d in range(1, n_y):
-                y_copies[d, k].wait_recv()
-                f_copies[d, k].start()
-
-        if k == last:
-            for d in range(1, n_y):
-                y_copies[d, k].wait_recv()
-        elif k >= tail:
-            pl.when(core == 1)(go)
+                y_copy(d, k, at).wait_recv()
+                if k < last:
+                    f_copy(d, k, at).start()
+
+        if last > k >= tail:
+            pl.when(core == 1)(lambda: go(cols(k)))
         else:
             sent(k, go)
 
@@ -320,13 +316,12 @@
         hit = jnp.dot(here, jnp.ones((nb, width), BF16), preferred_element_type=F32)
         out_v[rows_k, :] = jnp.where(hit > 0.5, 0.0, a_v[rows_k, :].astype(F32)).astype(BF16)
 
-    forward(0)
 
     pl.when(me == 0)(reduce_and_send)
-    forward(1)
-    forward(2)
-
-    late = [tail - 1] if tail - 1 > 2 else []
+    for k in range(min(2, tail)):
+        forward(k)
+
+    late = range(2, tail)
     far = (core == 1) | (me >= n_prow * 3 // 4)
     for k in late:
         pl.when(far)(functools.partial(forward, k))
@@ -349,25 +344,25 @@
     u_block = jnp.dot(inv_v[...], top_rows, preferred_element_type=F32).astype(BF16)
 
     def arrived(k):
-        def go():
+        def go(at):
             for d in range(1, n_y):
-                f_copies[d, k].wait_recv()
+                f_copy(d, k, at).wait_recv()
         if last > k >= tail:
-            pl.when(core == 0)(go)
+            pl.when(core == 0)(lambda: go(cols(k)))
         elif k < tail:
             sent(k, go)
 
-    def update(first, last):
-        for k in range(first, last):
+    def update(first, end, start=None):
+        for k in range(first, end):
             arrived(k)
-        start, stop = bounds[first], bounds[last]
+        start, stop = bounds[first] if start is None else start, bounds[end]
         rows_k = pl.ds(start, stop - start)
         panel = l_full[:, :, rows_k].reshape(nb, stop - start)
         product = lax.dot_general(
             panel, u_block, (((0,), (0,)), ((), ())), preferred_element_type=F32)
         out_v[rows_k, :] = (out_v[rows_k, :].astype(F32) - product).astype(BF16)
 
-    most = max(top, tail - 1)
+    most = max(1, tail - 1)
 
     @pl.when(me > 0)
     def _():
@@ -375,9 +370,8 @@
 
     @pl.when(me == 0)
     def _():
-        out_v[pl.ds(0, bounds[top]), :] = u_block[:bounds[top], :]
-        if most > top:
-            update(top, most)
+        out_v[pl.ds(0, nb), :] = u_block
+        update(0, most, nb)
 
     u_out[...] = u_block
     for k in range(tail + 1, last):
@@ -389,47 +383,28 @@
         arrived(k)
     forward(last)
 
-    @pl.when(me == 0)
-    def _():
-        arrive(origs.at[pl.ds(0, nb - piece)], o1_send)
-
-    m_copy.wait_send()
-    if_red(me, lambda: arrive(part.at[pl.ds(0, n_red - 1)], p1_send))
-    pl.when(jnp.logical_not(is_red(me)))(lambda: arrive(part, p1_send))
-
-    def drain():
-        @pl.when(me == 0)
-        def _():
-            arrive(got.at[pl.ds(1, n_prow - 1)], o2_send)
-
-        @pl.when(me > 0)
-        def _():
-            arrive(got.at[pl.ds(1, n_prow - 2)], o2_send)
-
-        arrive(got.at[pl.ds(1, n_prow - 1)], p2_send)
-
-    if_red(me, drain)
-
-    def sent_all(lanes, sem):
-        tiles = lanes * (n_y - 1) // 128
-        if tiles:
-            full = rows // 128
+    def drain(pieces):
+        while pieces:
+            some = min(pieces, rows // piece)
+            arrive(out_v.at[pl.ds(0, some * piece)], p1_send)
+            pieces -= some
+
+    pl.when(jnp.logical_not(is_red(me)))(lambda: drain(n_red))
+    pl.when(is_red(me) & (me > 0))(lambda: drain(n_red - 1 + n_prow - 1 + n_prow - 2))
+    pl.when(me == 0)(lambda: drain(2 * (n_red - 1) + 2 * (n_prow - 1)))
+
+    def sent_all(lanes):
+        tiles = (lanes * (n_y - 1) + rows) // 128
+        full = rows // 128
+        while tiles:
             count = next((n for n in range(1, n_pcol + 1) if tiles % n == 0 and tiles // n <= full), 0)
-            parts = [(count, tiles // count)] if count else [(tiles // full, full), (1, tiles % full)]
-            for count, wide in parts:
-                arrive(l_full.at[pl.ds(0, count), :, pl.ds(0, wide * 128)], sem)
-
-    shared, end = rows - bounds[tail], rows - bounds[last]
-    for skip, here in ((0, me > 0), (bounds[top], me == 0)):
-        @pl.when(here & (core == 0))
-        def _():
-            sent_all(bounds[tail] - skip, y_send)
-            sent_all(bounds[tail] - skip, f_send)
-
-        @pl.when(here & (core == 1))
-        def _():
-            sent_all(rows + shared + 2 * end - skip, y_send)
-            sent_all(rows + shared - 2 * end - skip, f_send)
+            count, wide = (count, tiles // count) if count else (min(n_pcol, tiles // full), full)
+            arrive(l_full.at[pl.ds(0, count), :, pl.ds(0, wide * 128)], y_send)
+            tiles -= count * wide
+
+    for skip, here in ((0, me > 0), (nb, me == 0)):
+        pl.when(here & (core == 0))(functools.partial(sent_all, 2 * (bounds[tail] - skip)))
+        pl.when(here & (core == 1))(functools.partial(sent_all, 2 * (2 * rows - bounds[tail] - skip)))
 
 
 def last_update(start, in_v, l_full, u_in, out_hbm, end_v, sem):
@@ -450,12 +425,12 @@
 
 def chunk_bounds(rows, nb):
     last = min(5 * nb, (rows - nb) // 2)
-    bounds = [0, nb]
+    bounds = [0, min(5 * nb, rows - last)]
     while bounds[-1] < rows - last:
         bounds.append(min(bounds[-1] + 4 * nb, rows - last))
     tail = len(bounds) - 1
     if last == 5 * nb:
-        bounds += [rows - 2 * nb, rows - nb // 2]
+        bounds += [rows - 5 * nb // 2, rows - nb]
     return (*bounds, rows), tail
 
 
@@ -489,8 +464,8 @@
             pltpu.VMEM((piece, width), BF16),
             pltpu.VMEM((nb, width), BF16),
             pltpu.VMEM((nb, width), BF16),
-            dma((2,)), dma((LOADS,)), dma((7,)), dma((5,)),
-            dma((max(n_y - 1, 1), chunks)), dma((max(n_y - 1, 1), chunks)), flag((3,)),
+            dma((2,)), dma((LOADS,)), dma((2,)), dma((5,)),
+            dma((max(n_y - 1, 1), chunks)), dma((max(n_y - 1, 1), max(chunks - 1, 1))), flag((3,)),
         ],
         compiler_params=pltpu.CompilerParams(
             collective_id=0, has_side_effects=True, vmem_limit_bytes=24 * 2 ** 20),

time: 16.2 us -> 16 us (0.988)
  Pallas kernels: 16 us -> 15.7 us
    pallas_call x1, Pallas kernels: 15 us -> 14.7 us  [body(): pl.pallas_call(functools.partial(kernel, n_prow, n_pcol, bounds, tail), o...]
where the time goes in v6:
time: 16 us; the launch traced here: 15.7 us
  Pallas kernels  15.7 us (98%)
    pallas_call x1, Pallas kernels, body(): pl.pallas_call(functools.partial(kernel, n_prow, n_pcol, bounds, tail), o...  14.7 us
    pallas_call x1, Pallas kernels, body(): pl.pallas_call(functools.partial(last_update, start), out_shape=jax.Shape...  0.98 us

profile of v6, /device:TPU:0, one launch (start us, length us, event | category | flops | bytes accessed | tf_op | source)
XLA Modules:
  0.0 15.7 jit_solution(4046495669204431718)
XLA Ops:
  0.0 14.7 %shard_map.46 = (bf16[4096,128]{1,0:T(8,128)(2,1)S(1)}, bf16[4,64,4096]{2,1,0:T(8,128)(2,1)S(1)}, bf16[256,128]{1,0:T(8,128)(2,1)S(1)}) custom-call(bf16[4096,128]{1,0:T(8,128)(2,1)} %a_hbm.1, bf16[64,4096]{1,0:T(8,128)(2,1)} %bitcast.2, bf16[256,256]{1,0:T(8,128)(2,1)} %inv_hbm.1, s32[1,256]{1,0:T(1,128)} %bitcast.3), custom_call_target="tpu_custom_call" | custom-call | tf_op jit(solution)/shard_map/pallas_call | solution.py:448
  14.7 1.0 %shard_map.47 = bf16[4096,128]{1,0:T(8,128)(2,1)} custom-call(bf16[4096,128]{1,0:T(8,128)(2,1)S(1)} %get-tuple-element.8.in_v, bf16[4,64,4096]{2,1,0:T(8,128)(2,1)S(1)} %get-tuple-element.9.l_full, bf16[256,128]{1,0:T(8,128)(2,1)S(1)} %get-tuple-element.10.u_in), custom_call_target="tpu_custom_call" | custom-call | tf_op jit(solution)/shard_map/pallas_call | solution.py:474

commit v7 on v6

--- a/solution.py
+++ b/solution.py
@@ -135,12 +135,13 @@
             src, dst, y_send, y_recv.at[d - 1, k], device_id=(me, y_peer(d)), device_id_type=MESH)
 
     last = chunks - 1
-    y_twice = [
-        pltpu.make_async_remote_copy(
-            both(y, last), both(y, last), y_send, y_recv.at[d - 1, last],
+    again_first = last - 1 if last - 1 > tail else last
+
+    def y_twice(d, k):
+        return pltpu.make_async_remote_copy(
+            both(y, k), both(y, k), y_send, y_recv.at[d - 1, k],
             device_id=(me, y_peer(d) - core), device_id_type=MESH)
-        for d in range(1, n_y)
-    ]
+
     m_copy = pltpu.make_async_remote_copy(
         l_hbm, l_full.at[col], m_send, m_recv, device_id=(me, mate), device_id_type=MESH)
 
@@ -232,8 +233,13 @@
     def _():
         for k in range(tail, chunks):
             for d in range(1, n_y):
+                if k == again_first:
+                    @pl.when(me == 0)
+                    def _():
+                        for j in range(again_first, chunks):
+                            y_twice(d, j).start()
                 if k == last:
-                    y_twice[d - 1].start()
+                    pl.when(me > 0)(lambda: y_twice(d, k).start())
                 y_copy(d, k, cols(k)).start()
 
     def f_copy(d, k, at):
@@ -250,7 +256,9 @@
         def go(at):
             for d in range(1, n_y):
                 y_copy(d, k, at).wait_recv()
-                if k < last:
+                if k == again_first < last:
+                    pl.when(me > 0)(lambda: f_copy(d, k, at).start())
+                elif k < last:
                     f_copy(d, k, at).start()
 
         if last > k >= tail:
@@ -346,7 +354,11 @@
     def arrived(k):
         def go(at):
             for d in range(1, n_y):
-                f_copy(d, k, at).wait_recv()
+                if k == again_first < last:
+                    pl.when(me > 0)(lambda: f_copy(d, k, at).wait_recv())
+                    pl.when(me == 0)(lambda: y_copy(d, k, at).wait_recv())
+                else:
+                    f_copy(d, k, at).wait_recv()
         if last > k >= tail:
             pl.when(core == 0)(lambda: go(cols(k)))
         elif k < tail:
@@ -430,7 +442,7 @@
         bounds.append(min(bounds[-1] + 4 * nb, rows - last))
     tail = len(bounds) - 1
     if last == 5 * nb:
-        bounds += [rows - 5 * nb // 2, rows - nb]
+        bounds += [rows - 5 * nb // 2, rows - nb, rows - nb // 2]
     return (*bounds, rows), tail
 
 

time: 16 us -> 16 us (level)
  no operation moved by 1% of the time
where the time goes in v7:
time: 16 us; the launch traced here: 15.7 us
  Pallas kernels  15.7 us (98%)
    pallas_call x1, Pallas kernels, body(): pl.pallas_call(functools.partial(kernel, n_prow, n_pcol, bounds, tail), o...  14.7 us
    pallas_call x1, Pallas kernels, body(): pl.pallas_call(functools.partial(last_update, start), out_shape=jax.Shape...  0.98 us

profile of v7, /device:TPU:0, one launch (start us, length us, event | category | flops | bytes accessed | tf_op | source)
XLA Modules:
  0.0 15.7 jit_solution(17459347876491611773)
XLA Ops:
  0.0 14.7 %shard_map.46 = (bf16[4096,128]{1,0:T(8,128)(2,1)S(1)}, bf16[4,64,4096]{2,1,0:T(8,128)(2,1)S(1)}, bf16[256,128]{1,0:T(8,128)(2,1)S(1)}) custom-call(bf16[4096,128]{1,0:T(8,128)(2,1)} %a_hbm.1, bf16[64,4096]{1,0:T(8,128)(2,1)} %bitcast.2, bf16[256,256]{1,0:T(8,128)(2,1)} %inv_hbm.1, s32[1,256]{1,0:T(1,128)} %bitcast.3), custom_call_target="tpu_custom_call" | custom-call | tf_op jit(solution)/shard_map/pallas_call | solution.py:460
  14.7 1.0 %shard_map.47 = bf16[4096,128]{1,0:T(8,128)(2,1)} custom-call(bf16[4096,128]{1,0:T(8,128)(2,1)S(1)} %get-tuple-element.8.in_v, bf16[4,64,4096]{2,1,0:T(8,128)(2,1)S(1)} %get-tuple-element.9.l_full, bf16[256,128]{1,0:T(8,128)(2,1)S(1)} %get-tuple-element.10.u_in), custom_call_target="tpu_custom_call" | custom-call | tf_op jit(solution)/shard_map/pallas_call | solution.py:486

commit v8 on v7

--- a/solution.py
+++ b/solution.py
@@ -291,7 +291,7 @@
                 device_id=(0, col), device_id_type=MESH).wait_recv()
 
         pl.semaphore_wait(rest_up, n_prow - n_red)
-        for d in range(1, n_prow):
+        for d in reversed(range(1, n_prow)):
             not_first(d, o2_copies[d].start)
 
     def arrive(ref, sem):
@@ -311,7 +311,7 @@
         tops[pl.ds(slot * piece, piece), :] = acc.astype(BF16)
         for d in range(1, n_prow):
             pl.when(me + d == n_prow)(p2_copies[d].start)
-        for d in range(1, n_prow):
+        for d in reversed(range(1, n_prow)):
             not_first(d, p2_copies[d].start)
 
     pl.when((me > 0) & is_red(me))(reduce_and_send)
@@ -330,7 +330,7 @@
         forward(k)
 
     late = range(2, tail)
-    far = (core == 1) | (me >= n_prow * 3 // 4)
+    far = (core == 1) | (me >= n_prow // 2)
     for k in late:
         pl.when(far)(functools.partial(forward, k))
 

time: 16 us -> 16.3 us (1.019)
  the two profiles are of different devices: /device:TPU:0 before, /device:TPU:17 now
where the time goes in v8:
time: 16.3 us; the launch traced here: 16.1 us
  Pallas kernels  16.1 us (99%)
    pallas_call x1, Pallas kernels, body(): pl.pallas_call(functools.partial(kernel, n_prow, n_pcol, bounds, tail), o...  15.1 us
    pallas_call x1, Pallas kernels, body(): pl.pallas_call(functools.partial(last_update, start), out_shape=jax.Shape...  0.98 us

profile of v8, /device:TPU:17, one launch (start us, length us, event | category | flops | bytes accessed | tf_op | source)
XLA Modules:
  0.0 16.1 jit_solution(13299994128774381810)
XLA Ops:
  0.0 15.1 %shard_map.46 = (bf16[4096,128]{1,0:T(8,128)(2,1)S(1)}, bf16[4,64,4096]{2,1,0:T(8,128)(2,1)S(1)}, bf16[256,128]{1,0:T(8,128)(2,1)S(1)}) custom-call(bf16[4096,128]{1,0:T(8,128)(2,1)} %a_hbm.1, bf16[64,4096]{1,0:T(8,128)(2,1)} %bitcast.2, bf16[256,256]{1,0:T(8,128)(2,1)} %inv_hbm.1, s32[1,256]{1,0:T(1,128)} %bitcast.3), custom_call_target="tpu_custom_call" | custom-call | tf_op jit(solution)/shard_map/pallas_call | solution.py:460
  15.1 1.0 %shard_map.47 = bf16[4096,128]{1,0:T(8,128)(2,1)} custom-call(bf16[4096,128]{1,0:T(8,128)(2,1)S(1)} %get-tuple-element.8.in_v, bf16[4,64,4096]{2,1,0:T(8,128)(2,1)S(1)} %get-tuple-element.9.l_full, bf16[256,128]{1,0:T(8,128)(2,1)S(1)} %get-tuple-element.10.u_in), custom_call_target="tpu_custom_call" | custom-call | tf_op jit(solution)/shard_map/pallas_call | solution.py:486
